TPU v7x, 8 devices: a whole 2x2x1 slice. The times are simulated.
8 devices in a mesh: dp: 1 (over z), tp: 8 (over y, x, core).
Axes of the slice: x: 2, y: 2, z: 1, core: 2. Of those that a mesh axis runs over, the one named last changes fastest.
Arguments:
- x_chunk: bfloat16 [8, 512, 4096], P('dp', 'tp')
- prefix_len: int32 [8], P('dp')
- k_cache: bfloat16 [8, 4096, 32, 128], P('dp', None, 'tp')
- v_cache: bfloat16 [8, 4096, 32, 128], P('dp', None, 'tp')
- ln1_gain: bfloat16 [4096], replicated
- ln1_bias: bfloat16 [4096], replicated
- w_qkv: bfloat16 [4096, 12288], P(None, 'tp')
- b_qkv: bfloat16 [12288], P('tp')
- w_out: bfloat16 [4096, 4096], P('tp')
- b_out: bfloat16 [4096], replicated
- ln2_gain: bfloat16 [4096], replicated
- ln2_bias: bfloat16 [4096], replicated
- w_up: bfloat16 [4096, 16384], P(None, 'tp')
- b_up: bfloat16 [16384], P('tp')
- w_down: bfloat16 [16384, 4096], P('tp')
- b_down: bfloat16 [4096], replicated
Outputs:
- output 1: bfloat16 [8, 512, 4096], P('dp', 'tp')
- output 2: bfloat16 [8, 4096, 32, 128], P('dp', None, 'tp')
- output 3: bfloat16 [8, 4096, 32, 128], P('dp', None, 'tp')
All inputs are finite; a program needn't handle non-finite values.
Results may differ from a plain program's by a relative error of at most 0.0125854.
Values are sent between devices in bfloat16 or wider.
A program may use at most 1 GiB of HBM per device.

v0:
```python
import jax
import jax.numpy as jnp
from jax import lax
from jax.sharding import PartitionSpec as P

LN_EPS = 1e-5


def layer_norm(tok_rows, ln_gain, ln_bias):
    rows_f32 = tok_rows.astype(jnp.float32)
    row_mean = jnp.mean(rows_f32, axis=-1, keepdims=True)
    centered = rows_f32 - row_mean
    row_var = jnp.mean(centered * centered, axis=-1, keepdims=True)
    normed = centered * lax.rsqrt(row_var + LN_EPS)
    return (normed * ln_gain.astype(jnp.float32) + ln_bias.astype(jnp.float32)).astype(jnp.bfloat16)


def write_rows(cache_seq, new_rows, start_pos):
    zero_idx = jnp.zeros_like(start_pos)
    return lax.dynamic_update_slice(cache_seq, new_rows, (start_pos, zero_idx, zero_idx))


def attend(queries, k_upd, v_upd, prefix_len, head_offset, heads_all):
    batch_n, chunk_len, heads_loc, head_dim = queries.shape
    cache_len = k_upd.shape[1]
    scores = jnp.einsum('bchd,bthd->bhct', queries, k_upd, preferred_element_type=jnp.float32) * (head_dim ** -0.5)
    head_ids = head_offset + jnp.arange(heads_loc)
    slopes = jnp.exp2(-8.0 * (head_ids + 1).astype(jnp.float32) / heads_all)
    query_pos = prefix_len[:, None] + jnp.arange(chunk_len)[None, :]
    rel_pos = (jnp.arange(cache_len)[None, None, :] - query_pos[:, :, None]).astype(jnp.float32)
    scores = scores + slopes[None, :, None, None] * rel_pos[:, None]
    scores = jnp.where((rel_pos <= 0.0)[:, None], scores, -1e30)
    attn_probs = jax.nn.softmax(scores, axis=-1).astype(jnp.bfloat16)
    context = jnp.einsum('bhct,bthd->bchd', attn_probs, v_upd, preferred_element_type=jnp.float32)
    return context.astype(jnp.bfloat16).reshape(batch_n, chunk_len, heads_loc * head_dim)


def solution(mesh):
    tp_size = mesh.shape['tp']

    def local_layer(x_local, prefix_len, k_cache, v_cache, ln1_gain, ln1_bias, w_qkv, b_qkv, w_out, b_out, ln2_gain, ln2_bias, w_up, b_up, w_down, b_down):
        batch_n, tok_loc = x_local.shape[0], x_local.shape[1]
        heads_loc, head_dim = k_cache.shape[2], k_cache.shape[3]
        chunk_len = tok_loc * tp_size
        normed = layer_norm(x_local, ln1_gain, ln1_bias)
        gathered = lax.all_gather(normed, 'tp', axis=1, tiled=True)
        qkv_proj = jnp.einsum('bcd,de->bce', gathered, w_qkv, preferred_element_type=jnp.float32) + b_qkv.astype(jnp.float32)
        qkv_heads = qkv_proj.astype(jnp.bfloat16).reshape(batch_n, chunk_len, heads_loc, 3, head_dim)
        k_upd = jax.vmap(write_rows)(k_cache, qkv_heads[:, :, :, 1], prefix_len)
        v_upd = jax.vmap(write_rows)(v_cache, qkv_heads[:, :, :, 2], prefix_len)
        head_offset = lax.axis_index('tp') * heads_loc
        context = attend(qkv_heads[:, :, :, 0], k_upd, v_upd, prefix_len, head_offset, heads_loc * tp_size)
        attn_part = jnp.einsum('bce,ed->bcd', context, w_out, preferred_element_type=jnp.float32).astype(jnp.bfloat16)
        attn_sum = lax.psum_scatter(attn_part, 'tp', scatter_dimension=1, tiled=True)
        residual = (x_local.astype(jnp.float32) + attn_sum.astype(jnp.float32) + b_out.astype(jnp.float32)).astype(jnp.bfloat16)
        normed2 = layer_norm(residual, ln2_gain, ln2_bias)
        gathered2 = lax.all_gather(normed2, 'tp', axis=1, tiled=True)
        up_pre = jnp.einsum('bcd,df->bcf', gathered2, w_up, preferred_element_type=jnp.float32) + b_up.astype(jnp.float32)
        up_act = jax.nn.gelu(up_pre, approximate=True).astype(jnp.bfloat16)
        down_part = jnp.einsum('bcf,fd->bcd', up_act, w_down, preferred_element_type=jnp.float32).astype(jnp.bfloat16)
        down_sum = lax.psum_scatter(down_part, 'tp', scatter_dimension=1, tiled=True)
        x_out = (residual.astype(jnp.float32) + down_sum.astype(jnp.float32) + b_down.astype(jnp.float32)).astype(jnp.bfloat16)
        return x_out, k_upd, v_upd

    tok_spec = P('dp', 'tp', None)
    cache_spec = P('dp', None, 'tp', None)
    replicated = P()
    in_specs = (tok_spec, P('dp'), cache_spec, cache_spec, replicated, replicated, P(None, 'tp'), P('tp'), P('tp', None), replicated, replicated, replicated, P(None, 'tp'), P('tp'), P('tp', None), replicated)
    return jax.shard_map(local_layer, mesh=mesh, in_specs=in_specs, out_specs=(tok_spec, cache_spec, cache_spec), check_vma=False)
```

profile of v0, /device:TPU:0, one launch (start us, length us, event | category | flops | bytes accessed | tf_op | source)
XLA Modules:
  0.0 1755.4 jit_solution(1591994145002093430)
XLA Ops:
  7.2 23.3 %copy.63 = bf16[8,4096,4,128]{3,2,1,0:T(4,128)(2,1)} copy(bf16[8,4096,4,128]{3,2,1,0:T(4,128)(2,1)} %param.18) | data formatting | bytes 67108864
  30.5 24.1 %copy.64 = bf16[8,4096,4,128]{3,2,1,0:T(4,128)(2,1)} copy(bf16[8,4096,4,128]{3,2,1,0:T(4,128)(2,1)} %param.19) | data formatting | bytes 67108864
  61.1 21.3 %subtract_convert_fusion = f32[8,512,4096]{2,1,0:T(8,128)} fusion(s32[8,512]{1,0:T(8,128)S(1)} %iota_add_fusion), kind=kLoop, calls=%fused_computation.21 | loop fusion | flops 33554432 | bytes 67125248 | tf_op jit(solution)/shard_map/convert_element_type | solution.py:30
  82.4 15.5 broadcast_compare_fusion
  97.9 120.4 %all-gather.3.cloned.1.call-done = bf16[8,512,4096]{2,1,0:T(8,128)(2,1)} async-done(((bf16[8,64,4096]{2,1,0:T(8,128)(2,1)}), bf16[8,512,4096]{2,1,0:T(8,128)(2,1)}) %all-gather.3.cloned.1.call-update) | async-done | bytes 33554448 | tf_op jit(solution)/shard_map/all_gather | solution.py:46
  218.3 60.3 %add_convert_fusion = bf16[8,512,1536]{2,1,0:T(8,128)(2,1)} fusion(bf16[8,512,4096]{2,1,0:T(8,128)(2,1)} %all-gather.3.cloned.1.call-done, bf16[4096,1536]{1,0:T(8,128)(2,1)} %param.22, f32[1536]{0:T(1024)S(1)} %convert_element_type.92), kind=kOutput, calls=%fused_computation.37 | convolution fusion | flops 51552190464 | bytes 58726400 | tf_op jit(solution)/shard_map/bcd,de->bce/dot_general | solution.py:47
  278.6 16.7 copy.25
  295.3 6.0 slice_bitcast_fusion.3
  301.3 72.7 %while.3 = (s32[]{:T(128)}, bf16[8,4096,4,128]{3,2,1,0:T(4,128)(2,1)}, s32[8,4]{0,1:T(4,128)S(1)}, bf16[8,512,4,128]{1,3,2,0:T(8,128)(2,1)}, s32[]{:T(128)}, /*index=5*/s32[4]{0:T(128)S(1)}) while((s32[]{:T(128)}, bf16[8,4096,4,128]{3,2,1,0:T(4,128)(2,1)}, s32[8,4]{0,1:T(4,128)S(1)}, bf16[8,512,4,128]{1,3,2,0:T(8,128)(2,1)}, s32[]{:T(128)}, ...), condition=%wide.while_cond.1, body=%wide.while_body.1.sunk | while | flops 262173 | bytes 3671726 | solution.py:20
  374.0 102.5 %fusion.19 = f32[8,4,512,4096]{3,2,1,0:T(8,128)} fusion(bf16[8,4096,4,128]{3,2,1,0:T(4,128)(2,1)} %get-tuple-element.16, bf16[8,512,4,3,128]{1,4,3,2,0:T(8,128)(2,1)} %bitcast.69), kind=kOutput, calls=%fused_computation.32 | convolution fusion | flops 17179869184 | bytes 306184192 | tf_op jit(solution)/shard_map/bchd,bthd->bhct/dot_general | solution.py:26
  476.6 75.3 %while.2 = (s32[]{:T(128)}, bf16[8,4096,4,128]{3,2,1,0:T(4,128)(2,1)}, s32[8,4]{0,1:T(4,128)S(1)}, bf16[8,512,4,128]{1,3,2,0:T(8,128)(2,1)}, s32[]{:T(128)}, /*index=5*/s32[4]{0:T(128)S(1)}) while((s32[]{:T(128)}, bf16[8,4096,4,128]{3,2,1,0:T(4,128)(2,1)}, s32[8,4]{0,1:T(4,128)S(1)}, bf16[8,512,4,128]{1,3,2,0:T(8,128)(2,1)}, s32[]{:T(128)}, ...), condition=%wide.while_cond, body=%wide.while_body.sunk | while | flops 262173 | bytes 3671726 | solution.py:20
  481.9 4.1 fusion.61
  491.3 4.1 fusion.61
  510.1 4.1 fusion.61
  551.9 351.2 %fusion.50 = (f32[8,4,512]{2,1,0:T(4,128)S(1)}, f32[8,4,512,4096]{3,2,1,0:T(8,128)}) fusion(f32[8,4,512,4096]{3,2,1,0:T(8,128)} %fusion.19, f32[8,512,4096]{2,1,0:T(8,128)} %subtract_convert_fusion, f32[4]{0:T(128)S(1)} %copy-done.13, pred[8,512,4096]{2,1,0:T(8,128)(4,1)} %broadcast_compare_fusion), kind=kOutput, calls=%fused_computation.82 | output fusion | flops 671092736 | bytes 620822528 | tf_op jit(solution)/shard_map/sub | solution.py:33
  903.1 93.6 %fusion.41 = bf16[8,4,128,512]{3,2,1,0:T(8,128)(2,1)} fusion(f32[8,4,512,4096]{3,2,1,0:T(8,128)} %get-tuple-element.56, f32[8,4,512]{2,1,0:T(4,128)S(1)} %get-tuple-element.55, bf16[8,4096,4,128]{3,2,1,0:T(4,128)(2,1)} %get-tuple-element.8), kind=kOutput, calls=%fused_computation.67 | convolution fusion | flops 17316184064 | bytes 306249728 | tf_op jit(solution)/shard_map/bhct,bthd->bchd/dot_general | solution.py:34
  996.6 24.0 %convolution_convert_fusion = bf16[8,512,4096]{2,1,0:T(8,128)(2,1)} fusion(bf16[8,512,512]{1,2,0:T(8,128)(2,1)} %bitcast.70, bf16[512,4096]{1,0:T(8,128)(2,1)} %param.24), kind=kOutput, calls=%fused_computation.35 | convolution fusion | flops 17196646400 | bytes 41943040 | tf_op jit(solution)/shard_map/bce,ed->bcd/dot_general | solution.py:53
  1021.4 195.6 %reduce-scatter.3.cloned.1.call-done = bf16[8,64,4096]{2,1,0:T(8,128)(2,1)} async-done(((bf16[8,512,4096]{2,1,0:T(8,128)(2,1)}), bf16[8,64,4096]{2,1,0:T(8,128)(2,1)}) %reduce-scatter.3.cloned.1.call-update) | async-done | bytes 4194320 | tf_op jit(solution)/shard_map/reduce_scatter | solution.py:54
  1217.0 5.4 convert_reduce_fusion
  1228.0 155.3 %all-gather.5.cloned.1.call-done = bf16[8,512,4096]{2,1,0:T(8,128)(2,1)} async-done(((bf16[8,64,4096]{2,1,0:T(8,128)(2,1)}), bf16[8,512,4096]{2,1,0:T(8,128)(2,1)}) %all-gather.5.cloned.1.call-update) | async-done | bytes 33554448 | tf_op jit(solution)/shard_map/all_gather | solution.py:57
  1383.3 84.1 %fusion.17 = bf16[8,512,2048]{2,1,0:T(8,128)(2,1)} fusion(bf16[8,512,4096]{2,1,0:T(8,128)(2,1)} %all-gather.5.cloned.1.call-done, bf16[4096,2048]{1,0:T(8,128)(2,1)} %param.28, f32[2048]{0:T(1024)S(1)} %convert_element_type.107), kind=kOutput, calls=%fused_computation.30 | convolution fusion | flops 68803362816 | bytes 67117056 | tf_op jit(solution)/shard_map/bcd,df->bcf/dot_general | solution.py:58
  1467.5 77.4 %convolution_convert_fusion.1 = bf16[8,512,4096]{2,1,0:T(8,128)(2,1)} fusion(bf16[8,512,2048]{2,1,0:T(8,128)(2,1)} %fusion.17, bf16[2048,4096]{1,0:T(8,128)(2,1)} %param.30), kind=kOutput, calls=%fused_computation.36 | convolution fusion | flops 68736253952 | bytes 67108864 | tf_op jit(solution)/shard_map/bcf,fd->bcd/dot_general | solution.py:60
  1545.6 195.7 %reduce-scatter.5.cloned.1.call-done = bf16[8,64,4096]{2,1,0:T(8,128)(2,1)} async-done(((bf16[8,512,4096]{2,1,0:T(8,128)(2,1)}), bf16[8,64,4096]{2,1,0:T(8,128)(2,1)}) %reduce-scatter.5.cloned.1.call-update) | async-done | bytes 4194320 | tf_op jit(solution)/shard_map/reduce_scatter | solution.py:61
  1741.3 7.4 fusion.39
  (152 shorter events, 148.9 us)
Async XLA Ops:
  7.2 211.1 %all-gather.3.cloned.1.call-start = ((), (), s32[]{:S(2)}) async-start(), calls=%async_computation.2 | async-start | bytes 37748736 | tf_op jit(solution)/shard_map/all_gather | solution.py:46
  30.5 24.2 %copy-start = (bf16[8,64,4096]{2,1,0:T(8,128)(2,1)S(1)}, bf16[8,64,4096]{2,1,0:T(8,128)(2,1)}, u32[]{:S(2)}) copy-start(bf16[8,64,4096]{2,1,0:T(8,128)(2,1)} %param.16) | copy-start | bytes 12582916
  30.5 26.1 %copy-start.3 = (bf16[4096]{0:T(1024)(128)(2,1)S(1)}, bf16[4096]{0:T(1024)(128)(2,1)}, u32[]{:S(2)}) copy-start(bf16[4096]{0:T(1024)(128)(2,1)} %param.20) | copy-start | bytes 24580
  30.5 26.1 %copy-start.4 = (bf16[4096]{0:T(1024)(128)(2,1)S(1)}, bf16[4096]{0:T(1024)(128)(2,1)}, u32[]{:S(2)}) copy-start(bf16[4096]{0:T(1024)(128)(2,1)} %param.21) | copy-start | bytes 24580
  54.7 5.6 copy-start.9
  54.7 6.2 copy-start.11
  54.7 6.2 copy-start.12
  60.1 1157.0 %reduce-scatter.3.cloned.1.call-start = ((), (), s32[]{:S(2)}) async-start(), calls=%async_computation.3 | async-start | bytes 37748736 | tf_op jit(solution)/shard_map/reduce_scatter | solution.py:54
  278.6 22.6 %copy-start.2 = (s32[4]{0:T(128)S(1)}, s32[4]{0:T(128)}, u32[]{:S(2)}) copy-start(s32[4]{0:T(128)} %constant.142) | copy-start | bytes 52
  476.6 75.3 %copy-start.13 = (f32[4]{0:T(128)S(1)}, f32[4]{0:T(128)}, u32[]{:S(2)}) copy-start(f32[4]{0:T(128)} %multiply_exponential_fusion) | copy-start | bytes 52
  1020.7 0.7 copy-start.5
  1020.7 0.7 copy-start.6
  1020.7 0.7 copy-start.7
  1020.7 207.3 %copy-start.10 = (bf16[2048]{0:T(1024)(128)(2,1)S(1)}, bf16[2048]{0:T(1024)(128)(2,1)}, u32[]{:S(2)}) copy-start(bf16[2048]{0:T(1024)(128)(2,1)} %param.29) | copy-start | bytes 12292
  1020.7 362.6 %all-gather.5.cloned.1.call-start = ((), (), s32[]{:S(2)}) async-start(), calls=%async_computation.4 | async-start | bytes 37748736 | tf_op jit(solution)/shard_map/all_gather | solution.py:57
  1222.5 2.0 copy-start.1
  1228.0 513.3 %reduce-scatter.5.cloned.1.call-start = ((), (), s32[]{:S(2)}) async-start(), calls=%async_computation.5 | async-start | bytes 37748736 | tf_op jit(solution)/shard_map/reduce_scatter | solution.py:61
  1544.9 0.7 copy-start.8
Sparse Core Ops, SparseCore 0:
  60.2 158.0 all-gather.2
  1020.8 196.1 reduce-scatter.2
  1228.1 155.2 all-gather.4
  1545.1 196.1 reduce-scatter.4
where the time goes:
time: 1760 us
  waiting for transfers between devices  667 us (38%)
  other arithmetic  527 us (30%)
  matrix products  442 us (25%)
  local copies, waits for them, and re-layouts  105 us (6%)
    sub x1, other arithmetic, attend(): attn_probs = jax.nn.softmax(scores, axis=-1).astype(jnp.bfloat16)  351 us
    reduce_scatter x1, waiting for transfers between devices, local_layer(): lax.psum_scatter(down_part, 'tp', scatter_dimension=1, tiled=True)  196 us
    reduce_scatter x1, waiting for transfers between devices, local_layer(): lax.psum_scatter(attn_part, 'tp', scatter_dimension=1, tiled=True)  196 us
    all_gather x1, waiting for transfers between devices, local_layer(): gathered2 = lax.all_gather(normed2, 'tp', axis=1, tiled=True)  155 us
    all_gather x1, waiting for transfers between devices, local_layer(): gathered = lax.all_gather(normed, 'tp', axis=1, tiled=True)  120 us
    scatter x32, other arithmetic  115 us
    dot_general x1, matrix products, attend(): jnp.einsum('bchd,bthd->bhct', queries, k_upd, preferred_element_type=jnp....  103 us
    dot_general x1, matrix products, attend(): jnp.einsum('bhct,bthd->bchd', attn_probs, v_upd, preferred_element_type=j...  93.6 us
  transfers between devices with their start and end apart: 4, of which 4 were waited for; matrix products, arithmetic and copies ran while one was open for 2% of the time, Pallas kernels for 0%

commit v1 on v0

v1 whole, which is shorter than its diff:
```python
import functools

import jax
import jax.numpy as jnp
from jax import lax
from jax.experimental import pallas as pl
from jax.experimental.pallas import tpu as pltpu
from jax.sharding import PartitionSpec as P

LN_EPS = 1e-5
LOG2E = 1.4426950408889634
N_CHUNKS = 4
KV_BLOCK = 512
PAIR_FIRST = True


def norm_rows(rows_f32, gain_ref, bias_ref):
    row_mean = jnp.mean(rows_f32, axis=-1, keepdims=True)
    centered = rows_f32 - row_mean
    row_var = jnp.mean(centered * centered, axis=-1, keepdims=True)
    normed = centered * lax.rsqrt(row_var + LN_EPS)
    return (normed * gain_ref[...].astype(jnp.float32) + bias_ref[...].astype(jnp.float32)).astype(jnp.bfloat16)


def norm_kernel(x_ref, gain_ref, bias_ref, out_ref):
    out_ref[0] = norm_rows(x_ref[0].astype(jnp.float32), gain_ref, bias_ref)


def add_norm_kernel(x_ref, sum_ref, b_ref, gain_ref, bias_ref, res_ref, out_ref):
    res = (x_ref[0].astype(jnp.float32) + sum_ref[0].astype(jnp.float32) + b_ref[...].astype(jnp.float32)).astype(jnp.bfloat16)
    res_ref[0] = res
    out_ref[0] = norm_rows(res.astype(jnp.float32), gain_ref, bias_ref)


def add_kernel(x_ref, sum_ref, b_ref, *refs):
    refs[-1][0] = (x_ref[0].astype(jnp.float32) + sum_ref[0].astype(jnp.float32) + b_ref[...].astype(jnp.float32)).astype(jnp.bfloat16)


def copy_kernel(after_ref, k_ref, v_ref, k_out, v_out):
    k_out[...] = k_ref[...]
    v_out[...] = v_ref[...]


def copy_caches(k_rows, v_rows, after):
    batch_n, rows, head_dim = k_rows.shape
    block = min(4096, rows)
    spec = pl.BlockSpec((1, block, head_dim), lambda b, i: (b, i, 0))
    shape = jax.ShapeDtypeStruct(k_rows.shape, k_rows.dtype)
    return pl.pallas_call(
        copy_kernel, grid=(batch_n, rows // block), in_specs=[pl.BlockSpec(memory_space=pl.ANY), spec, spec], out_specs=[spec, spec],
        out_shape=[shape, shape], name="copy_caches",
        cost_estimate=pl.CostEstimate(flops=k_rows.size * 4, bytes_accessed=k_rows.size * 8, transcendentals=0),
    )(after, k_rows, v_rows)


def row_specs(first_seq, tok_loc, d_model):
    whole = pl.BlockSpec((1, tok_loc, d_model), lambda i: (first_seq + i, 0, 0))
    own = pl.BlockSpec((1, tok_loc, d_model), lambda i: (i, 0, 0))
    vec = pl.BlockSpec((1, d_model), lambda i: (0, 0))
    return whole, own, vec


def norm_chunk(x_local, gain, bias, first_seq, seqs):
    _, tok_loc, d_model = x_local.shape
    whole, own, vec = row_specs(first_seq, tok_loc, d_model)
    size = seqs * tok_loc * d_model
    return pl.pallas_call(
        norm_kernel, grid=(seqs,), in_specs=[whole, vec, vec], out_specs=own,
        out_shape=jax.ShapeDtypeStruct((seqs, tok_loc, d_model), jnp.bfloat16),
        cost_estimate=pl.CostEstimate(flops=size * 20, bytes_accessed=size * 4, transcendentals=0), name="norm_in",
    )(x_local, gain, bias)


def add_norm_chunk(x_local, summed, b, gain, bias, first_seq, seqs):
    _, tok_loc, d_model = x_local.shape
    whole, own, vec = row_specs(first_seq, tok_loc, d_model)
    size = seqs * tok_loc * d_model
    shape = jax.ShapeDtypeStruct((seqs, tok_loc, d_model), jnp.bfloat16)
    return pl.pallas_call(
        add_norm_kernel, grid=(seqs,), in_specs=[whole, own, vec, vec, vec], out_specs=[own, own], out_shape=[shape, shape],
        cost_estimate=pl.CostEstimate(flops=size * 24, bytes_accessed=size * 8, transcendentals=0), name="add_norm",
    )(x_local, summed, b, gain, bias)


def add_chunk(res, summed, b, prev, first_seq, batch_n):
    seqs, tok_loc, d_model = res.shape
    whole, own, vec = row_specs(first_seq, tok_loc, d_model)
    size = seqs * tok_loc * d_model
    args, specs, aliases = [res, summed, b], [own, own, vec], {}
    if prev is not None:
        args.append(prev)
        specs.append(pl.BlockSpec(memory_space=pl.ANY))
        aliases = {3: 0}
    return pl.pallas_call(
        add_kernel, grid=(seqs,), in_specs=specs, out_specs=whole, input_output_aliases=aliases,
        out_shape=jax.ShapeDtypeStruct((batch_n, tok_loc, d_model), jnp.bfloat16),
        cost_estimate=pl.CostEstimate(flops=size * 4, bytes_accessed=size * 6, transcendentals=0), name="add_out",
    )(*args)


def attn_kernel(heads_loc, head_dim, block, first_seq, len_ref, slope_ref, qkv_ref, k_ref, v_ref, ctx_ref, kn_ref, vn_ref, k32, v32, m_s, l_s, acc_s):
    step = pl.program_id(1)
    start = len_ref[first_seq + pl.program_id(0)]
    chunk = qkv_ref.shape[1]
    scale = head_dim ** -0.5 * LOG2E
    contract_last = (((1,), (1,)), ((), ()))
    contract = (((1,), (0,)), ((), ()))

    @pl.when(step == 0)
    def _():
        row = lax.broadcasted_iota(jnp.int32, (chunk, chunk), 0)
        col = lax.broadcasted_iota(jnp.int32, (chunk, chunk), 1)
        col_f = lax.broadcasted_iota(jnp.int32, (1, chunk), 1).astype(jnp.float32)

        def head(h, carry):
            base = pl.multiple_of(h * (3 * head_dim), head_dim)
            q = qkv_ref[0, :, pl.ds(base, head_dim)]
            k = qkv_ref[0, :, pl.ds(base + head_dim, head_dim)]
            v = qkv_ref[0, :, pl.ds(base + 2 * head_dim, head_dim)]
            k32[pl.ds(h, chunk, stride=heads_loc), :] = k.astype(jnp.float32)
            v32[pl.ds(h, chunk, stride=heads_loc), :] = v.astype(jnp.float32)
            s = lax.dot_general(q, k, contract_last, preferred_element_type=jnp.float32) * scale
            s = s + slope_ref[h] * col_f
            s = jnp.where(col <= row, s, -1e30)
            m = jnp.max(s, axis=1, keepdims=True)
            p = jnp.exp2(s - m)
            m_s[h] = jnp.broadcast_to(m, (chunk, head_dim))
            l_s[h] = jnp.broadcast_to(jnp.sum(p, axis=1, keepdims=True), (chunk, head_dim))
            acc_s[h] = lax.dot_general(p.astype(jnp.bfloat16), v, contract, preferred_element_type=jnp.float32)
            return carry

        lax.fori_loop(0, heads_loc, head, 0)
        kn_ref[0] = k32[...].astype(jnp.bfloat16)
        vn_ref[0] = v32[...].astype(jnp.bfloat16)

    first = (step - 1) * block

    @pl.when((step > 0) & (first < start))
    def _():
        k32[...] = k_ref[0].astype(jnp.float32)
        v32[...] = v_ref[0].astype(jnp.float32)
        pos_col = first + lax.broadcasted_iota(jnp.int32, (block, head_dim), 0)
        pos = first + lax.broadcasted_iota(jnp.int32, (1, block), 1)
        rel = (pos - start).astype(jnp.float32)

        def head(h, carry):
            base = pl.multiple_of(h * (3 * head_dim), head_dim)
            q = qkv_ref[0, :, pl.ds(base, head_dim)]
            k = k32[pl.ds(h, block, stride=heads_loc), :]
            k = jnp.where(pos_col < start, k, 0.0).astype(jnp.bfloat16)
            v = v32[pl.ds(h, block, stride=heads_loc), :].astype(jnp.bfloat16)
            bias = jnp.where(pos < start, slope_ref[h] * rel, -1e30)
            s = lax.dot_general(q, k, contract_last, preferred_element_type=jnp.float32) * scale + bias
            m_old = m_s[h]
            m_new = jnp.maximum(m_old, jnp.max(s, axis=1, keepdims=True))
            p = jnp.exp2(s - jnp.tile(m_new, (1, block // head_dim)))
            alpha = jnp.exp2(m_old - m_new)
            m_s[h] = m_new
            l_s[h] = l_s[h] * alpha + jnp.sum(p, axis=1, keepdims=True)
            acc_s[h] = acc_s[h] * alpha + lax.dot_general(p.astype(jnp.bfloat16), v, contract, preferred_element_type=jnp.float32)
            return carry

        lax.fori_loop(0, heads_loc, head, 0)

    @pl.when(step == pl.num_programs(1) - 1)
    def _():
        for h in range(heads_loc):
            ctx_ref[0, :, h * head_dim:(h + 1) * head_dim] = (acc_s[h] / l_s[h]).astype(jnp.bfloat16)


def attention(qkv, k_rows, v_rows, prefix_len, slopes, first_seq, heads_loc, head_dim, cache_len):
    seqs, chunk, width = qkv.shape
    block = KV_BLOCK
    blocks = pl.cdiv(cache_len - chunk, block)

    def kv_map(b, j, lens, sl):
        last = jnp.maximum((lens[first_seq + b] + block - 1) // block - 1, 0)
        return (first_seq + b, jnp.clip(j - 1, 0, last), 0)

    kv_spec = pl.BlockSpec((1, block * heads_loc, head_dim), kv_map)
    new_spec = pl.BlockSpec((1, chunk * heads_loc, head_dim), lambda b, j, lens, sl: (b, 0, 0))
    rows_max = max(block, chunk) * heads_loc
    macs = 2 * seqs * chunk * cache_len * heads_loc * head_dim
    return pl.pallas_call(
        functools.partial(attn_kernel, heads_loc, head_dim, block, first_seq),
        grid_spec=pltpu.PrefetchScalarGridSpec(
            num_scalar_prefetch=2,
            grid=(seqs, blocks + 1),
            in_specs=[pl.BlockSpec((1, chunk, width), lambda b, j, lens, sl: (b, 0, 0)), kv_spec, kv_spec],
            out_specs=[pl.BlockSpec((1, chunk, heads_loc * head_dim), lambda b, j, lens, sl: (b, 0, 0)), new_spec, new_spec],
            scratch_shapes=[
                pltpu.VMEM((rows_max, head_dim), jnp.float32),
                pltpu.VMEM((rows_max, head_dim), jnp.float32),
                pltpu.VMEM((heads_loc, chunk, head_dim), jnp.float32),
                pltpu.VMEM((heads_loc, chunk, head_dim), jnp.float32),
                pltpu.VMEM((heads_loc, chunk, head_dim), jnp.float32),
            ],
        ),
        out_shape=[
            jax.ShapeDtypeStruct((seqs, chunk, heads_loc * head_dim), jnp.bfloat16),
            jax.ShapeDtypeStruct((seqs, chunk * heads_loc, head_dim), jnp.bfloat16),
            jax.ShapeDtypeStruct((seqs, chunk * heads_loc, head_dim), jnp.bfloat16),
        ],
        compiler_params=pltpu.CompilerParams(dimension_semantics=("arbitrary", "arbitrary")),
        cost_estimate=pl.CostEstimate(flops=2 * macs, bytes_accessed=4 * seqs * cache_len * heads_loc * head_dim, transcendentals=0),
        name="prefill_attention",
    )(prefix_len, slopes, qkv, k_rows, v_rows)


def solution(mesh):
    tp_size = mesh.shape['tp']

    def local_layer(x_local, prefix_len, k_cache, v_cache, ln1_gain, ln1_bias, w_qkv, b_qkv, w_out, b_out, ln2_gain, ln2_bias, w_up, b_up, w_down, b_down):
        batch_n, tok_loc, d_model = x_local.shape
        cache_len, heads_loc, head_dim = k_cache.shape[1:]
        chunk_len = tok_loc * tp_size
        head_ids = lax.axis_index('tp') * heads_loc + jnp.arange(heads_loc)
        slopes = jnp.exp2(-8.0 * (head_ids + 1).astype(jnp.float32) / (heads_loc * tp_size)) * LOG2E
        k_rows = k_cache.reshape(batch_n, cache_len * heads_loc, head_dim)
        v_rows = v_cache.reshape(batch_n, cache_len * heads_loc, head_dim)
        seqs = batch_n // N_CHUNKS
        core = lax.axis_index('tp') % 2
        pairs = [(i, i ^ 1) for i in range(tp_size)]
        same_core = [[i for i in range(tp_size) if i % 2 == c] for c in range(2)]
        vecs = [v.reshape(1, d_model) for v in (ln1_gain, ln1_bias, b_out, ln2_gain, ln2_bias, b_down)]
        gain1, bias1, bias_out, gain2, bias2, bias_down = vecs

        def gather(rows):
            return lax.all_gather(rows, 'tp', axis=1, tiled=True)

        def reduce_scatter(acts, weights):
            if not PAIR_FIRST:
                part = jnp.einsum('bce,ed->bcd', acts, weights, preferred_element_type=jnp.float32).astype(jnp.bfloat16)
                return lax.psum_scatter(part, 'tp', scatter_dimension=1, tiled=True)
            by_core = acts.reshape(seqs, tp_size // 2, 2, tok_loc, acts.shape[-1])

            def half(which):
                mine = lax.dynamic_index_in_dim(by_core, which, axis=2, keepdims=False).reshape(seqs, chunk_len // 2, acts.shape[-1])
                return jnp.einsum('bce,ed->bcd', mine, weights, preferred_element_type=jnp.float32)

            other = lax.ppermute(half(1 - core).astype(jnp.bfloat16), 'tp', pairs)
            part = (half(core) + other.astype(jnp.float32)).astype(jnp.bfloat16)
            return lax.psum_scatter(part, 'tp', scatter_dimension=1, tiled=True, axis_index_groups=same_core)

        normed = [norm_chunk(x_local, gain1, bias1, c * seqs, seqs) for c in range(N_CHUNKS)]
        k_upd, v_upd = (rows.reshape(k_cache.shape) for rows in copy_caches(k_rows, v_rows, normed[-1]))
        gathered = [gather(rows) for rows in normed]
        contexts = []
        for c in range(N_CHUNKS):
            qkv = (jnp.einsum('bcd,de->bce', gathered[c], w_qkv, preferred_element_type=jnp.float32) + b_qkv.astype(jnp.float32)).astype(jnp.bfloat16)
            context, k_new, v_new = attention(qkv, k_rows, v_rows, prefix_len, slopes, c * seqs, heads_loc, head_dim, cache_len)
            contexts.append(context)
            k_new = k_new.reshape(seqs, chunk_len, heads_loc, head_dim)
            v_new = v_new.reshape(seqs, chunk_len, heads_loc, head_dim)
            for b in range(seqs):
                at = (c * seqs + b, prefix_len[c * seqs + b], 0, 0)
                k_upd = lax.dynamic_update_slice(k_upd, k_new[b:b + 1], at)
                v_upd = lax.dynamic_update_slice(v_upd, v_new[b:b + 1], at)
        x_out = None
        for c in range(N_CHUNKS):
            attn_sum = reduce_scatter(contexts[c], w_out)
            residual, normed2 = add_norm_chunk(x_local, attn_sum, bias_out, gain2, bias2, c * seqs, seqs)
            up_pre = jnp.einsum('bcd,df->bcf', gather(normed2), w_up, preferred_element_type=jnp.float32) + b_up.astype(jnp.float32)
            up_act = jax.nn.gelu(up_pre, approximate=True).astype(jnp.bfloat16)
            x_out = add_chunk(residual, reduce_scatter(up_act, w_down), bias_down, x_out, c * seqs, batch_n)
        return x_out, k_upd, v_upd

    tok_spec = P('dp', 'tp', None)
    cache_spec = P('dp', None, 'tp', None)
    replicated = P()
    in_specs = (tok_spec, P('dp'), cache_spec, cache_spec, replicated, replicated, P(None, 'tp'), P('tp'), P('tp', None), replicated, replicated, replicated, P(None, 'tp'), P('tp'), P('tp', None), replicated)
    return jax.shard_map(local_layer, mesh=mesh, in_specs=in_specs, out_specs=(tok_spec, cache_spec, cache_spec), check_vma=False)
```

time: 1760 us -> 844 us (0.48)
  other arithmetic: 527 us -> 0.53 us
  waiting for transfers between devices: 667 us -> 227 us
  Pallas kernels: 0 us -> 216 us
  matrix products: 442 us -> 322 us
  local copies, waits for them, and re-layouts: 105 us -> 35 us
    sub x1 -> x0, other arithmetic: 351 us -> none  [attend(): attn_probs = jax.nn.softmax(scores, axis=-1).astype(jnp.bfloat16)]
    reduce_scatter x2 -> x8, waiting for transfers between devices: 391 us -> 60.7 us  [reduce_scatter(): lax.psum_scatter(part, 'tp', scatter_dimension=1, tiled=True, axis_index_...]
    pallas_call x0 -> x17, Pallas kernels: none -> 216 us  [the longest x4 126 us: attention(): pl.pallas_call(functools.partial(attn_kernel, heads_loc, head_dim, block,...]
    all_gather x2 -> x8, waiting for transfers between devices: 276 us -> 122 us  [gather(): return lax.all_gather(rows, 'tp', axis=1, tiled=True)]
    dot_general x6 -> x24, matrix products: 442 us -> 322 us  [the longest x16 145 us: half(): jnp.einsum('bce,ed->bcd', mine, weights, preferred_element_type=jnp.float32)]
    scatter x33 -> x0, other arithmetic: 115 us -> none
    unnamed x31 -> x40, local copies, waits for them, and re-layouts: 49.1 us -> 0.08 us
    ppermute x0 -> x8, waiting for transfers between devices: none -> 44.7 us  [reduce_scatter(): other = lax.ppermute(half(1 - core).astype(jnp.bfloat16), 'tp', pairs)]
  transfers between devices with their start and end apart: 4 -> 24, of which waited for: 4 -> 12; matrix products, arithmetic and copies ran while one was open for 2% -> 43% of each run, Pallas kernels for 0% -> 25%
where the time goes in v1:
time: 844 us; the launch traced here: 835 us
  matrix products  322 us (38%)
  waiting for transfers between devices  227 us (27%)
  Pallas kernels  216 us (26%)
  local copies, waits for them, and re-layouts  35 us (4%)
  between operations  30 us (4%)
    dot_general x16, matrix products, half(): jnp.einsum('bce,ed->bcd', mine, weights, preferred_element_type=jnp.float32)  145 us
    pallas_call x4, Pallas kernels, attention(): pl.pallas_call(functools.partial(attn_kernel, heads_loc, head_dim, block,...  126 us
    all_gather x8, waiting for transfers between devices, gather(): return lax.all_gather(rows, 'tp', axis=1, tiled=True)  122 us
    dot_general x4, matrix products, local_layer(): jnp.einsum('bcd,df->bcf', gather(normed2), w_up, preferred_element_type=j...  101 us
    dot_general x4, matrix products, local_layer(): jnp.einsum('bcd,de->bce', gathered[c], w_qkv, preferred_element_type=jnp....  76.6 us
    reduce_scatter x8, waiting for transfers between devices, reduce_scatter(): lax.psum_scatter(part, 'tp', scatter_dimension=1, tiled=True, axis_index_...  60.7 us
    pallas_call x1, Pallas kernels, copy_caches(): pl.pallas_call(copy_kernel, grid=(batch_n, rows // block), in_specs=[pl.B...  53.6 us
    ppermute x8, waiting for transfers between devices, reduce_scatter(): other = lax.ppermute(half(1 - core).astype(jnp.bfloat16), 'tp', pairs)  44.7 us
  transfers between devices with their start and end apart: 24, of which 12 were waited for; matrix products, arithmetic and copies ran while one was open for 43% of the time, Pallas kernels for 25%

profile of v1, /device:TPU:0, one launch (start us, length us, event | category | flops | bytes accessed | tf_op | source)
XLA Modules:
  0.0 835.0 jit_solution(13941959304934315194)
XLA Ops:
  22.6 41.6 %all-gather.17.cloned.1.call-done = bf16[2,512,4096]{2,1,0:T(8,128)(2,1)} async-done(((bf16[2,64,4096]{2,1,0:T(8,128)(2,1)}), bf16[2,512,4096]{2,1,0:T(8,128)(2,1)}) %all-gather.17.cloned.1.call-update) | async-done | bytes 8388624 | tf_op jit(solution)/shard_map/all_gather | solution.py:229
  64.1 19.1 %add_convert_fusion.9.qkv_ref = bf16[2,512,1536]{2,1,0:T(8,128)(2,1)} fusion(bf16[2,512,4096]{2,1,0:T(8,128)(2,1)} %all-gather.17.cloned.1.call-done, bf16[4096,1536]{1,0:T(8,128)(2,1)} %param.22, f32[1536]{0:T(1024)S(1)} %convert_element_type.112), kind=kOutput, calls=%fused_computation.77 | convolution fusion | flops 12888047616 | bytes 24123392 | tf_op jit(solution)/shard_map/bcd,de->bce/dot_general | solution.py:250
  83.3 34.9 %prefill_attention.6 = (bf16[2,512,512]{2,1,0:T(8,128)(2,1)}, bf16[2,2048,128]{2,1,0:T(8,128)(2,1)}, bf16[2,2048,128]{2,1,0:T(8,128)(2,1)}) custom-call(s32[8]{0:T(128)} %len_ref.7, f32[4]{0:T(128)} %exponential_multiply_fusion.slope_ref, bf16[2,512,1536]{2,1,0:T(8,128)(2,1)} %add_convert_fusion.9.qkv_ref, bf16[8,16384,128]{2,1,0:T(8,128)(2,1)} %bitcast.168, ...), custom_call_target="tpu_custom_call" | custom-call | flops 8589934592 | bytes 16777216 | tf_op jit(solution)/shard_map/prefill_attention/pallas_call | solution.py:184
  136.2 19.1 %add_convert_fusion.8.qkv_ref = bf16[2,512,1536]{2,1,0:T(8,128)(2,1)} fusion(bf16[2,512,4096]{2,1,0:T(8,128)(2,1)} %all-gather.21.cloned.1.call-done, bf16[4096,1536]{1,0:T(8,128)(2,1)} %param.22, f32[1536]{0:T(1024)S(1)} %convert_element_type.112), kind=kOutput, calls=%fused_computation.76 | convolution fusion | flops 12888047616 | bytes 24123392 | tf_op jit(solution)/shard_map/bcd,de->bce/dot_general | solution.py:250
  155.3 24.3 %prefill_attention.7 = (bf16[2,512,512]{2,1,0:T(8,128)(2,1)}, bf16[2,2048,128]{2,1,0:T(8,128)(2,1)}, bf16[2,2048,128]{2,1,0:T(8,128)(2,1)}) custom-call(s32[8]{0:T(128)} %len_ref.7, f32[4]{0:T(128)} %exponential_multiply_fusion.slope_ref, bf16[2,512,1536]{2,1,0:T(8,128)(2,1)} %add_convert_fusion.8.qkv_ref, bf16[8,16384,128]{2,1,0:T(8,128)(2,1)} %bitcast.169, ...), custom_call_target="tpu_custom_call" | custom-call | flops 8589934592 | bytes 16777216 | tf_op jit(solution)/shard_map/prefill_attention/pallas_call | solution.py:184
  200.9 19.2 %add_convert_fusion.10.qkv_ref = bf16[2,512,1536]{2,1,0:T(8,128)(2,1)} fusion(bf16[2,512,4096]{2,1,0:T(8,128)(2,1)} %all-gather.13.cloned.1.call-done, bf16[4096,1536]{1,0:T(8,128)(2,1)} %param.22, f32[1536]{0:T(1024)S(1)} %convert_element_type.112), kind=kOutput, calls=%fused_computation.78 | convolution fusion | flops 12888047616 | bytes 24123392 | tf_op jit(solution)/shard_map/bcd,de->bce/dot_general | solution.py:250
  220.1 32.4 %prefill_attention.5 = (bf16[2,512,512]{2,1,0:T(8,128)(2,1)}, bf16[2,2048,128]{2,1,0:T(8,128)(2,1)}, bf16[2,2048,128]{2,1,0:T(8,128)(2,1)}) custom-call(s32[8]{0:T(128)} %len_ref.7, f32[4]{0:T(128)} %exponential_multiply_fusion.slope_ref, bf16[2,512,1536]{2,1,0:T(8,128)(2,1)} %add_convert_fusion.10.qkv_ref, bf16[8,16384,128]{2,1,0:T(8,128)(2,1)} %bitcast.170, ...), custom_call_target="tpu_custom_call" | custom-call | flops 8589934592 | bytes 16777216 | tf_op jit(solution)/shard_map/prefill_attention/pallas_call | solution.py:184
  270.4 19.1 %add_convert_fusion.11.qkv_ref = bf16[2,512,1536]{2,1,0:T(8,128)(2,1)} fusion(bf16[2,512,4096]{2,1,0:T(8,128)(2,1)} %all-gather.9.cloned.1.call-done, bf16[4096,1536]{1,0:T(8,128)(2,1)} %param.22, f32[1536]{0:T(1024)S(1)} %convert_element_type.112), kind=kOutput, calls=%fused_computation.79 | convolution fusion | flops 12888047616 | bytes 24123392 | tf_op jit(solution)/shard_map/bcd,de->bce/dot_general | solution.py:250
  289.6 34.3 %prefill_attention.4 = (bf16[2,512,512]{2,1,0:T(8,128)(2,1)}, bf16[2,2048,128]{2,1,0:T(8,128)(2,1)}, bf16[2,2048,128]{2,1,0:T(8,128)(2,1)}) custom-call(s32[8]{0:T(128)} %len_ref.7, f32[4]{0:T(128)} %exponential_multiply_fusion.slope_ref, bf16[2,512,1536]{2,1,0:T(8,128)(2,1)} %add_convert_fusion.11.qkv_ref, bf16[8,16384,128]{2,1,0:T(8,128)(2,1)} %bitcast.171, ...), custom_call_target="tpu_custom_call" | custom-call | flops 8589934592 | bytes 16777216 | tf_op jit(solution)/shard_map/prefill_attention/pallas_call | solution.py:184
  350.9 14.5 %reduce-scatter.13.cloned.1.call-done.sum_ref = bf16[2,64,4096]{2,1,0:T(8,128)(2,1)} async-done(((bf16[2,256,4096]{2,1,0:T(8,128)(2,1)}), bf16[2,64,4096]{2,1,0:T(8,128)(2,1)}) %reduce-scatter.13.cloned.1.call-update) | async-done | bytes 1048592 | tf_op jit(solution)/shard_map/reduce_scatter | solution.py:243
  369.4 46.2 %reduce-scatter.9.cloned.1.call-done.sum_ref = bf16[2,64,4096]{2,1,0:T(8,128)(2,1)} async-done(((bf16[2,256,4096]{2,1,0:T(8,128)(2,1)}), bf16[2,64,4096]{2,1,0:T(8,128)(2,1)}) %reduce-scatter.9.cloned.1.call-update) | async-done | bytes 1048592 | tf_op jit(solution)/shard_map/reduce_scatter | solution.py:243
  419.3 47.1 %all-gather.19.cloned.1.call-done = bf16[2,512,4096]{2,1,0:T(8,128)(2,1)} async-done(((bf16[2,64,4096]{2,1,0:T(8,128)(2,1)}), bf16[2,512,4096]{2,1,0:T(8,128)(2,1)}) %all-gather.19.cloned.1.call-update) | async-done | bytes 8388624 | tf_op jit(solution)/shard_map/all_gather | solution.py:229
  466.4 25.5 %fusion.55 = bf16[2,512,2048]{2,1,0:T(8,128)(2,1)} fusion(f32[2048]{0:T(1024)S(1)} %convert_element_type.117, bf16[2,512,4096]{2,1,0:T(8,128)(2,1)} %all-gather.19.cloned.1.call-done, bf16[4096,2048]{1,0:T(8,128)(2,1)} %param.28), kind=kOutput, calls=%fused_computation.59 | convolution fusion | flops 17200840704 | bytes 29368320 | tf_op jit(solution)/shard_map/bcd,df->bcf/dot_general | solution.py:263
  491.9 24.5 %all-gather.23.cloned.1.call-done = bf16[2,512,4096]{2,1,0:T(8,128)(2,1)} async-done(((bf16[2,64,4096]{2,1,0:T(8,128)(2,1)}), bf16[2,512,4096]{2,1,0:T(8,128)(2,1)}) %all-gather.23.cloned.1.call-update) | async-done | bytes 8388624 | tf_op jit(solution)/shard_map/all_gather | solution.py:229
  516.5 24.7 %fusion.63 = bf16[2,512,2048]{2,1,0:T(8,128)(2,1)S(1)} fusion(f32[2048]{0:T(1024)S(1)} %convert_element_type.117, bf16[2,512,4096]{2,1,0:T(8,128)(2,1)} %all-gather.23.cloned.1.call-done, bf16[4096,2048]{1,0:T(8,128)(2,1)} %param.28), kind=kOutput, calls=%fused_computation.67 | convolution fusion | flops 17200840704 | bytes 29368320 | tf_op jit(solution)/shard_map/bcd,df->bcf/dot_general | solution.py:263
  555.4 13.9 %fusion.70 = bf16[2,256,4096]{2,1,0:T(8,128)(2,1)} fusion(bf16[2,256,2048]{2,1,0:T(8,128)(2,1)S(1)} %bitcast.187, bf16[2048,4096]{1,0:T(8,128)(2,1)} %param.30), kind=kOutput, calls=%fused_computation.86 | convolution fusion | flops 8592031744 | bytes 23068672 | tf_op jit(solution)/shard_map/bce,ed->bcd/dot_general | solution.py:239
  569.6 13.9 %add_convert_fusion = bf16[2,256,4096]{2,1,0:T(8,128)(2,1)} fusion(bf16[2,256,4096]{2,1,0:T(8,128)(2,1)S(1)} %collective-permute-done.7, bf16[2,256,2048]{2,1,0:T(8,128)(2,1)S(1)} %bitcast.185, bf16[2048,4096]{1,0:T(8,128)(2,1)} %param.30), kind=kOutput, calls=%fused_computation.68 | convolution fusion | flops 8596226048 | bytes 27262976 | tf_op jit(solution)/shard_map/bce,ed->bcd/dot_general | solution.py:239
  583.6 25.5 %fusion.47 = bf16[2,512,2048]{2,1,0:T(8,128)(2,1)} fusion(f32[2048]{0:T(1024)S(1)} %convert_element_type.117, bf16[2,512,4096]{2,1,0:T(8,128)(2,1)} %all-gather.15.cloned.1.call-done, bf16[4096,2048]{1,0:T(8,128)(2,1)} %param.28), kind=kOutput, calls=%fused_computation.51 | convolution fusion | flops 17200840704 | bytes 29368320 | tf_op jit(solution)/shard_map/bcd,df->bcf/dot_general | solution.py:263
  617.4 25.5 %fusion.39 = bf16[2,512,2048]{2,1,0:T(8,128)(2,1)} fusion(f32[2048]{0:T(1024)S(1)} %convert_element_type.117, bf16[2,512,4096]{2,1,0:T(8,128)(2,1)} %all-gather.11.cloned.1.call-done, bf16[4096,2048]{1,0:T(8,128)(2,1)} %param.28), kind=kOutput, calls=%fused_computation.43 | convolution fusion | flops 17200840704 | bytes 29368320 | tf_op jit(solution)/shard_map/bcd,df->bcf/dot_general | solution.py:263
  642.9 14.4 %add_convert_fusion.2 = bf16[2,256,4096]{2,1,0:T(8,128)(2,1)} fusion(bf16[2,256,4096]{2,1,0:T(8,128)(2,1)} %collective-permute-done.5, bf16[2,256,2048]{2,1,0:T(8,128)(2,1)S(1)} %bitcast.182, bf16[2048,4096]{1,0:T(8,128)(2,1)} %param.30), kind=kOutput, calls=%fused_computation.70 | convolution fusion | flops 8596226048 | bytes 27262976 | tf_op jit(solution)/shard_map/bce,ed->bcd/dot_general | solution.py:239
  683.1 13.9 %add_convert_fusion.4 = bf16[2,256,4096]{2,1,0:T(8,128)(2,1)} fusion(bf16[2,256,4096]{2,1,0:T(8,128)(2,1)S(1)} %collective-permute-done.3, bf16[2,256,2048]{2,1,0:T(8,128)(2,1)S(1)} %bitcast.186, bf16[2048,4096]{1,0:T(8,128)(2,1)} %param.30), kind=kOutput, calls=%fused_computation.72 | convolution fusion | flops 8596226048 | bytes 27262976 | tf_op jit(solution)/shard_map/bce,ed->bcd/dot_general | solution.py:239
  697.1 13.3 %fusion.64 = bf16[2,256,4096]{2,1,0:T(8,128)(2,1)S(1)} fusion(bf16[2,256,2048]{2,1,0:T(8,128)(2,1)} %bitcast.184, bf16[2048,4096]{1,0:T(8,128)(2,1)} %param.30), kind=kOutput, calls=%fused_computation.84 | convolution fusion | flops 8592031744 | bytes 23068672 | tf_op jit(solution)/shard_map/bce,ed->bcd/dot_general | solution.py:239
  717.5 14.0 %add_convert_fusion.6 = bf16[2,256,4096]{2,1,0:T(8,128)(2,1)} fusion(bf16[2,256,4096]{2,1,0:T(8,128)(2,1)S(1)} %collective-permute-done.1, bf16[2,256,2048]{2,1,0:T(8,128)(2,1)S(1)} %bitcast.183, bf16[2048,4096]{1,0:T(8,128)(2,1)} %param.30), kind=kOutput, calls=%fused_computation.74 | convolution fusion | flops 8596226048 | bytes 27262976 | tf_op jit(solution)/shard_map/bce,ed->bcd/dot_general | solution.py:239
  748.1 53.6 %copy_caches.1 = (bf16[8,16384,128]{2,1,0:T(8,128)(2,1)}, bf16[8,16384,128]{2,1,0:T(8,128)(2,1)}) custom-call(bf16[2,64,4096]{2,1,0:T(8,128)(2,1)} %norm_in.4.after_ref, bf16[8,16384,128]{2,1,0:T(8,128)(2,1)} %bitcast.172, bf16[8,16384,128]{2,1,0:T(8,128)(2,1)} %bitcast.177), custom_call_target="tpu_custom_call" | custom-call | flops 67108864 | bytes 134217728 | tf_op jit(solution)/shard_map/copy_caches/pallas_call | solution.py:49
  (157 shorter events, 190.2 us)
Async XLA Ops:
  7.2 57.0 %all-gather.17.cloned.1.call-start = ((), (), s32[]{:S(2)}) async-start(), calls=%async_computation.16 | async-start | bytes 9437184 | tf_op jit(solution)/shard_map/all_gather | solution.py:229
  12.8 123.4 %all-gather.21.cloned.1.call-start = ((), (), s32[]{:S(2)}) async-start(), calls=%async_computation.20 | async-start | bytes 9437184 | tf_op jit(solution)/shard_map/all_gather | solution.py:229
  15.9 185.0 %all-gather.13.cloned.1.call-start = ((), (), s32[]{:S(2)}) async-start(), calls=%async_computation.12 | async-start | bytes 9437184 | tf_op jit(solution)/shard_map/all_gather | solution.py:229
  18.9 251.5 %all-gather.9.cloned.1.call-start = ((), (), s32[]{:S(2)}) async-start(), calls=%async_computation.8 | async-start | bytes 9437184 | tf_op jit(solution)/shard_map/all_gather | solution.py:229
  21.9 321.6 %reduce-scatter.17.cloned.1.call-start = ((), (), s32[]{:S(2)}) async-start(), calls=%async_computation.17 | async-start | bytes 5242880 | tf_op jit(solution)/shard_map/reduce_scatter | solution.py:243
  124.3 7.2 collective-permute-start.4
  135.9 211.3 %reduce-scatter.21.cloned.1.call-start = ((), (), s32[]{:S(2)}) async-start(), calls=%async_computation.21 | async-start | bytes 5242880 | tf_op jit(solution)/shard_map/reduce_scatter | solution.py:243
  185.7 10.4 %collective-permute-start.6 = (bf16[2,256,4096]{2,1,0:T(8,128)(2,1)S(1)}, bf16[2,256,4096]{2,1,0:T(8,128)(2,1)S(1)}, u32[]{:S(2)}, u32[]{:S(2)}) collective-permute-start(bf16[2,256,4096]{2,1,0:T(8,128)(2,1)S(1)} %convolution_convert_fusion), channel_id=1, source_target_pairs={{0,1},{1,0},{2,3},{3,2},{4,5},{5,4},{6,7},{7,6}} | collective-permute-start | bytes 12582920 | tf_op jit(solution)/shard_map/ppermute | solution.py:241
  200.4 164.9 %reduce-scatter.13.cloned.1.call-start = ((), (), s32[]{:S(2)}) async-start(), calls=%async_computation.13 | async-start | bytes 5242880 | tf_op jit(solution)/shard_map/reduce_scatter | solution.py:243
  258.6 7.2 collective-permute-start.2
  270.2 145.5 %reduce-scatter.9.cloned.1.call-start = ((), (), s32[]{:S(2)}) async-start(), calls=%async_computation.9 | async-start | bytes 5242880 | tf_op jit(solution)/shard_map/reduce_scatter | solution.py:243
  330.0 7.2 collective-permute-start
  341.6 124.8 %all-gather.19.cloned.1.call-start = ((), (), s32[]{:S(2)}) async-start(), calls=%async_computation.18 | async-start | bytes 9437184 | tf_op jit(solution)/shard_map/all_gather | solution.py:229
  347.1 169.4 %all-gather.23.cloned.1.call-start = ((), (), s32[]{:S(2)}) async-start(), calls=%async_computation.22 | async-start | bytes 9437184 | tf_op jit(solution)/shard_map/all_gather | solution.py:229
  350.8 232.8 %all-gather.15.cloned.1.call-start = ((), (), s32[]{:S(2)}) async-start(), calls=%async_computation.14 | async-start | bytes 9437184 | tf_op jit(solution)/shard_map/all_gather | solution.py:229
  368.9 248.4 %all-gather.11.cloned.1.call-start = ((), (), s32[]{:S(2)}) async-start(), calls=%async_computation.10 | async-start | bytes 9437184 | tf_op jit(solution)/shard_map/all_gather | solution.py:229
  419.3 398.7 %reduce-scatter.23.cloned.1.call-start = ((), (), s32[]{:S(2)}) async-start(), calls=%async_computation.23 | async-start | bytes 5242880 | tf_op jit(solution)/shard_map/reduce_scatter | solution.py:243
  555.2 14.4 %collective-permute-start.7 = (bf16[2,256,4096]{2,1,0:T(8,128)(2,1)S(1)}, bf16[2,256,4096]{2,1,0:T(8,128)(2,1)S(1)}, u32[]{:S(2)}, u32[]{:S(2)}) collective-permute-start(bf16[2,256,4096]{2,1,0:T(8,128)(2,1)S(1)} %fusion.73), channel_id=1, source_target_pairs={{0,1},{1,0},{2,3},{3,2},{4,5},{5,4},{6,7},{7,6}} | collective-permute-start | bytes 12582920 | tf_op jit(solution)/shard_map/ppermute | solution.py:241
  569.3 73.6 %collective-permute-start.5 = (bf16[2,256,4096]{2,1,0:T(8,128)(2,1)}, bf16[2,256,4096]{2,1,0:T(8,128)(2,1)}, u32[]{:S(2)}, u32[]{:S(2)}) collective-permute-start(bf16[2,256,4096]{2,1,0:T(8,128)(2,1)} %fusion.70), channel_id=1, source_target_pairs={{0,1},{1,0},{2,3},{3,2},{4,5},{5,4},{6,7},{7,6}} | collective-permute-start | bytes 12582920 | tf_op jit(solution)/shard_map/ppermute | solution.py:241
  583.5 236.9 %reduce-scatter.19.cloned.1.call-start = ((), (), s32[]{:S(2)}) async-start(), calls=%async_computation.19 | async-start | bytes 5242880 | tf_op jit(solution)/shard_map/reduce_scatter | solution.py:243
  657.3 165.6 %reduce-scatter.15.cloned.1.call-start = ((), (), s32[]{:S(2)}) async-start(), calls=%async_computation.15 | async-start | bytes 5242880 | tf_op jit(solution)/shard_map/reduce_scatter | solution.py:243
  675.9 7.2 collective-permute-start.3
  697.0 128.5 %reduce-scatter.11.cloned.1.call-start = ((), (), s32[]{:S(2)}) async-start(), calls=%async_computation.11 | async-start | bytes 5242880 | tf_op jit(solution)/shard_map/reduce_scatter | solution.py:243
  710.4 7.2 collective-permute-start.1
  (20 other events, 318.2 us)
Sparse Core Ops, SparseCore 0:
  12.9 51.1 all-gather.16
  65.9 48.3 all-gather.20
  116.7 48.3 all-gather.12
  166.8 48.3 all-gather.8
  218.5 46.8 reduce-scatter.16
  268.1 46.8 reduce-scatter.20
  318.4 46.8 reduce-scatter.12
  368.8 46.8 reduce-scatter.8
  418.1 48.3 all-gather.18
  468.1 48.3 all-gather.22
  518.3 48.3 all-gather.14
  569.0 48.3 all-gather.10
  620.3 46.8 reduce-scatter.22
  669.9 46.8 reduce-scatter.18
  719.5 46.8 reduce-scatter.14
  769.1 46.8 reduce-scatter.10

commit v2 on v1

--- a/solution.py
+++ b/solution.py
@@ -10,6 +10,7 @@
 LN_EPS = 1e-5
 LOG2E = 1.4426950408889634
 N_CHUNKS = 4
+MLP_GROUPS = 2
 KV_BLOCK = 512
 PAIR_FIRST = True
 
@@ -228,24 +229,26 @@
         def gather(rows):
             return lax.all_gather(rows, 'tp', axis=1, tiled=True)
 
-        def reduce_scatter(acts, weights):
+        def reduce_scatter(acts, weights, held=None):
             if not PAIR_FIRST:
                 part = jnp.einsum('bce,ed->bcd', acts, weights, preferred_element_type=jnp.float32).astype(jnp.bfloat16)
                 return lax.psum_scatter(part, 'tp', scatter_dimension=1, tiled=True)
-            by_core = acts.reshape(seqs, tp_size // 2, 2, tok_loc, acts.shape[-1])
+            by_core = acts.reshape(acts.shape[0], tp_size // 2, 2, tok_loc, acts.shape[-1])
 
             def half(which):
-                mine = lax.dynamic_index_in_dim(by_core, which, axis=2, keepdims=False).reshape(seqs, chunk_len // 2, acts.shape[-1])
+                mine = lax.dynamic_index_in_dim(by_core, which, axis=2, keepdims=False).reshape(acts.shape[0], chunk_len // 2, acts.shape[-1])
                 return jnp.einsum('bce,ed->bcd', mine, weights, preferred_element_type=jnp.float32)
 
             other = lax.ppermute(half(1 - core).astype(jnp.bfloat16), 'tp', pairs)
             part = (half(core) + other.astype(jnp.float32)).astype(jnp.bfloat16)
+            if held is not None:
+                part, held[0] = lax.optimization_barrier((part, held[0]))
             return lax.psum_scatter(part, 'tp', scatter_dimension=1, tiled=True, axis_index_groups=same_core)
 
         normed = [norm_chunk(x_local, gain1, bias1, c * seqs, seqs) for c in range(N_CHUNKS)]
         k_upd, v_upd = (rows.reshape(k_cache.shape) for rows in copy_caches(k_rows, v_rows, normed[-1]))
         gathered = [gather(rows) for rows in normed]
-        contexts = []
+        contexts, writes = [], []
         for c in range(N_CHUNKS):
             qkv = (jnp.einsum('bcd,de->bce', gathered[c], w_qkv, preferred_element_type=jnp.float32) + b_qkv.astype(jnp.float32)).astype(jnp.bfloat16)
             context, k_new, v_new = attention(qkv, k_rows, v_rows, prefix_len, slopes, c * seqs, heads_loc, head_dim, cache_len)
@@ -254,15 +257,27 @@
             v_new = v_new.reshape(seqs, chunk_len, heads_loc, head_dim)
             for b in range(seqs):
                 at = (c * seqs + b, prefix_len[c * seqs + b], 0, 0)
-                k_upd = lax.dynamic_update_slice(k_upd, k_new[b:b + 1], at)
-                v_upd = lax.dynamic_update_slice(v_upd, v_new[b:b + 1], at)
-        x_out = None
+                writes.append((k_new[b:b + 1], v_new[b:b + 1], at))
+        residuals, normed2 = [], []
         for c in range(N_CHUNKS):
             attn_sum = reduce_scatter(contexts[c], w_out)
-            residual, normed2 = add_norm_chunk(x_local, attn_sum, bias_out, gain2, bias2, c * seqs, seqs)
-            up_pre = jnp.einsum('bcd,df->bcf', gather(normed2), w_up, preferred_element_type=jnp.float32) + b_up.astype(jnp.float32)
+            residual, rows = add_norm_chunk(x_local, attn_sum, bias_out, gain2, bias2, c * seqs, seqs)
+            residuals.append(residual)
+            normed2.append(rows)
+        x_out = None
+        per_group = N_CHUNKS // MLP_GROUPS
+        groups = [slice(g * per_group, (g + 1) * per_group) for g in range(MLP_GROUPS)]
+        residuals = [jnp.concatenate(residuals[members], axis=0) for members in groups]
+        later = [gather(jnp.concatenate(normed2[members], axis=0)) for members in groups]
+        later[0], k_upd, v_upd = lax.optimization_barrier((later[0], k_upd, v_upd))
+        for k_new, v_new, at in writes:
+            k_upd = lax.dynamic_update_slice(k_upd, k_new, at)
+            v_upd = lax.dynamic_update_slice(v_upd, v_new, at)
+        for g in range(MLP_GROUPS):
+            rows = later.pop(0)
+            up_pre = jnp.einsum('bcd,df->bcf', rows, w_up, preferred_element_type=jnp.float32) + b_up.astype(jnp.float32)
             up_act = jax.nn.gelu(up_pre, approximate=True).astype(jnp.bfloat16)
-            x_out = add_chunk(residual, reduce_scatter(up_act, w_down), bias_down, x_out, c * seqs, batch_n)
+            x_out = add_chunk(residuals[g], reduce_scatter(up_act, w_down, later if later else None), bias_down, x_out, g * per_group * seqs, batch_n)
         return x_out, k_upd, v_upd
 
     tok_spec = P('dp', 'tp', None)

time: 844 us -> 827 us (0.980)
  matrix products: 322 us -> 295 us
  other arithmetic: 0.53 us -> 9.8 us
    all_gather x8 -> x6, waiting for transfers between devices: 122 us -> 74.2 us  [gather(): return lax.all_gather(rows, 'tp', axis=1, tiled=True)]
    reduce_scatter x8 -> x6, waiting for transfers between devices: 60.7 us -> 102 us  [reduce_scatter(): lax.psum_scatter(part, 'tp', scatter_dimension=1, tiled=True, axis_index_...]
    dot_general x16 -> x12, matrix products: 145 us -> 130 us  [half(): jnp.einsum('bce,ed->bcd', mine, weights, preferred_element_type=jnp.float32)]
    dot_general x4 -> x2, matrix products: 101 us -> 88.6 us  [local_layer(): jnp.einsum('bcd,df->bcf', rows, w_up, preferred_element_type=jnp.float32)]
    concatenate x0 -> x4, other arithmetic: none -> 9.18 us  [the longest x2 6.11 us: local_layer(): jnp.concatenate(normed2[members], axis=0)]
    ppermute x8 -> x6, waiting for transfers between devices: 44.7 us -> 47.9 us  [reduce_scatter(): other = lax.ppermute(half(1 - core).astype(jnp.bfloat16), 'tp', pairs)]
  transfers between devices with their start and end apart: 24 -> 18, of which waited for: 12 -> 11; matrix products, arithmetic and copies ran while one was open for 43% -> 41% of each run, Pallas kernels for 25% -> 26%
where the time goes in v2:
time: 827 us; the launch traced here: 813 us
  matrix products  295 us (36%)
  waiting for transfers between devices  224 us (27%)
  Pallas kernels  216 us (26%)
  local copies, waits for them, and re-layouts  34.1 us (4%)
  between operations  30.5 us (4%)
  other arithmetic  9.8 us (1%)
    dot_general x12, matrix products, half(): jnp.einsum('bce,ed->bcd', mine, weights, preferred_element_type=jnp.float32)  130 us
    pallas_call x4, Pallas kernels, attention(): pl.pallas_call(functools.partial(attn_kernel, heads_loc, head_dim, block,...  128 us
    reduce_scatter x6, waiting for transfers between devices, reduce_scatter(): lax.psum_scatter(part, 'tp', scatter_dimension=1, tiled=True, axis_index_...  102 us
    dot_general x2, matrix products, local_layer(): jnp.einsum('bcd,df->bcf', rows, w_up, preferred_element_type=jnp.float32)  88.6 us
    dot_general x4, matrix products, local_layer(): jnp.einsum('bcd,de->bce', gathered[c], w_qkv, preferred_element_type=jnp....  76.8 us
    all_gather x6, waiting for transfers between devices, gather(): return lax.all_gather(rows, 'tp', axis=1, tiled=True)  74.2 us
    pallas_call x1, Pallas kernels, copy_caches(): pl.pallas_call(copy_kernel, grid=(batch_n, rows // block), in_specs=[pl.B...  53.4 us
    ppermute x6, waiting for transfers between devices, reduce_scatter(): other = lax.ppermute(half(1 - core).astype(jnp.bfloat16), 'tp', pairs)  47.9 us
  transfers between devices with their start and end apart: 18, of which 11 were waited for; matrix products, arithmetic and copies ran while one was open for 41% of the time, Pallas kernels for 26%

profile of v2, /device:TPU:0, one launch (start us, length us, event | category | flops | bytes accessed | tf_op | source)
XLA Modules:
  0.0 813.2 jit_solution(9972225439423522956)
XLA Ops:
  22.6 41.5 %all-gather.13.cloned.1.call-done = bf16[2,512,4096]{2,1,0:T(8,128)(2,1)} async-done(((bf16[2,64,4096]{2,1,0:T(8,128)(2,1)}), bf16[2,512,4096]{2,1,0:T(8,128)(2,1)}) %all-gather.13.cloned.1.call-update) | async-done | bytes 8388624 | tf_op jit(solution)/shard_map/all_gather | solution.py:230
  64.1 19.1 %add_convert_fusion.6.qkv_ref = bf16[2,512,1536]{2,1,0:T(8,128)(2,1)} fusion(bf16[2,512,4096]{2,1,0:T(8,128)(2,1)} %all-gather.13.cloned.1.call-done, bf16[4096,1536]{1,0:T(8,128)(2,1)} %param.22, f32[1536]{0:T(1024)S(1)} %convert_element_type.86), kind=kOutput, calls=%fused_computation.46 | convolution fusion | flops 12888047616 | bytes 24123392 | tf_op jit(solution)/shard_map/bcd,de->bce/dot_general | solution.py:253
  83.2 24.3 %prefill_attention.7 = (bf16[2,512,512]{2,1,0:T(8,128)(2,1)}, bf16[2,2048,128]{2,1,0:T(8,128)(2,1)}, bf16[2,2048,128]{2,1,0:T(8,128)(2,1)}) custom-call(s32[8]{0:T(128)} %len_ref.7, f32[4]{0:T(128)} %exponential_multiply_fusion.slope_ref, bf16[2,512,1536]{2,1,0:T(8,128)(2,1)} %add_convert_fusion.6.qkv_ref, bf16[8,16384,128]{2,1,0:T(8,128)(2,1)} %bitcast.132, ...), custom_call_target="tpu_custom_call" | custom-call | flops 8589934592 | bytes 16777216 | tf_op jit(solution)/shard_map/prefill_attention/pallas_call | solution.py:185
  107.5 7.3 all-gather.11.cloned.1.call-done
  114.9 19.1 %add_convert_fusion.7.qkv_ref = bf16[2,512,1536]{2,1,0:T(8,128)(2,1)} fusion(bf16[2,512,4096]{2,1,0:T(8,128)(2,1)} %all-gather.11.cloned.1.call-done, bf16[4096,1536]{1,0:T(8,128)(2,1)} %param.22, f32[1536]{0:T(1024)S(1)} %convert_element_type.86), kind=kOutput, calls=%fused_computation.47 | convolution fusion | flops 12888047616 | bytes 24123392 | tf_op jit(solution)/shard_map/bcd,de->bce/dot_general | solution.py:253
  134.0 37.4 %prefill_attention.6 = (bf16[2,512,512]{2,1,0:T(8,128)(2,1)}, bf16[2,2048,128]{2,1,0:T(8,128)(2,1)}, bf16[2,2048,128]{2,1,0:T(8,128)(2,1)}) custom-call(s32[8]{0:T(128)} %len_ref.7, f32[4]{0:T(128)} %exponential_multiply_fusion.slope_ref, bf16[2,512,1536]{2,1,0:T(8,128)(2,1)} %add_convert_fusion.7.qkv_ref, bf16[8,16384,128]{2,1,0:T(8,128)(2,1)} %bitcast.133, ...), custom_call_target="tpu_custom_call" | custom-call | flops 8589934592 | bytes 16777216 | tf_op jit(solution)/shard_map/prefill_attention/pallas_call | solution.py:185
  177.8 6.9 collective-permute-done.3
  195.9 19.3 %add_convert_fusion.8.qkv_ref = bf16[2,512,1536]{2,1,0:T(8,128)(2,1)} fusion(bf16[2,512,4096]{2,1,0:T(8,128)(2,1)} %all-gather.9.cloned.1.call-done, bf16[4096,1536]{1,0:T(8,128)(2,1)} %param.22, f32[1536]{0:T(1024)S(1)} %convert_element_type.86), kind=kOutput, calls=%fused_computation.48 | convolution fusion | flops 12888047616 | bytes 24123392 | tf_op jit(solution)/shard_map/bcd,de->bce/dot_general | solution.py:253
  222.0 19.3 %add_convert_fusion.9.qkv_ref = bf16[2,512,1536]{2,1,0:T(8,128)(2,1)} fusion(bf16[2,512,4096]{2,1,0:T(8,128)(2,1)} %all-gather.7.cloned.1.call-done, bf16[4096,1536]{1,0:T(8,128)(2,1)} %param.22, f32[1536]{0:T(1024)S(1)} %convert_element_type.86), kind=kOutput, calls=%fused_computation.49 | convolution fusion | flops 12888047616 | bytes 24123392 | tf_op jit(solution)/shard_map/bcd,de->bce/dot_general | solution.py:253
  241.3 31.8 %prefill_attention.5 = (bf16[2,512,512]{2,1,0:T(8,128)(2,1)}, bf16[2,2048,128]{2,1,0:T(8,128)(2,1)}, bf16[2,2048,128]{2,1,0:T(8,128)(2,1)}) custom-call(s32[8]{0:T(128)} %len_ref.7, f32[4]{0:T(128)} %exponential_multiply_fusion.slope_ref, bf16[2,512,1536]{2,1,0:T(8,128)(2,1)} %add_convert_fusion.8.qkv_ref, bf16[8,16384,128]{2,1,0:T(8,128)(2,1)} %bitcast.134, ...), custom_call_target="tpu_custom_call" | custom-call | flops 8589934592 | bytes 16777216 | tf_op jit(solution)/shard_map/prefill_attention/pallas_call | solution.py:185
  273.2 34.5 %prefill_attention.4 = (bf16[2,512,512]{2,1,0:T(8,128)(2,1)}, bf16[2,2048,128]{2,1,0:T(8,128)(2,1)}, bf16[2,2048,128]{2,1,0:T(8,128)(2,1)}) custom-call(s32[8]{0:T(128)} %len_ref.7, f32[4]{0:T(128)} %exponential_multiply_fusion.slope_ref, bf16[2,512,1536]{2,1,0:T(8,128)(2,1)} %add_convert_fusion.9.qkv_ref, bf16[8,16384,128]{2,1,0:T(8,128)(2,1)} %bitcast.135, ...), custom_call_target="tpu_custom_call" | custom-call | flops 8589934592 | bytes 16777216 | tf_op jit(solution)/shard_map/prefill_attention/pallas_call | solution.py:185
  354.0 18.3 %reduce-scatter.9.cloned.1.call-done.sum_ref = bf16[2,64,4096]{2,1,0:T(8,128)(2,1)} async-done(((bf16[2,256,4096]{2,1,0:T(8,128)(2,1)}), bf16[2,64,4096]{2,1,0:T(8,128)(2,1)}) %reduce-scatter.9.cloned.1.call-update) | async-done | bytes 1048592 | tf_op jit(solution)/shard_map/reduce_scatter | solution.py:246
  375.9 46.8 %reduce-scatter.7.cloned.1.call-done.sum_ref = bf16[2,64,4096]{2,1,0:T(8,128)(2,1)} async-done(((bf16[2,256,4096]{2,1,0:T(8,128)(2,1)}), bf16[2,64,4096]{2,1,0:T(8,128)(2,1)}) %reduce-scatter.7.cloned.1.call-update) | async-done | bytes 1048592 | tf_op jit(solution)/shard_map/reduce_scatter | solution.py:246
  429.8 53.4 %copy_caches.1 = (bf16[8,16384,128]{2,1,0:T(8,128)(2,1)}, bf16[8,16384,128]{2,1,0:T(8,128)(2,1)}) custom-call(bf16[2,64,4096]{2,1,0:T(8,128)(2,1)} %norm_in.5.after_ref, bf16[8,16384,128]{2,1,0:T(8,128)(2,1)} %bitcast.136, bf16[8,16384,128]{2,1,0:T(8,128)(2,1)} %bitcast.141), custom_call_target="tpu_custom_call" | custom-call | flops 67108864 | bytes 134217728 | tf_op jit(solution)/shard_map/copy_caches/pallas_call | solution.py:50
  483.3 25.4 %all-gather.15.cloned.1.call-done = bf16[4,512,4096]{2,1,0:T(8,128)(2,1)} async-done(((bf16[4,64,4096]{2,1,0:T(8,128)(2,1)}), bf16[4,512,4096]{2,1,0:T(8,128)(2,1)}) %all-gather.15.cloned.1.call-update) | async-done | bytes 16777232 | tf_op jit(solution)/shard_map/all_gather | solution.py:230
  508.6 44.3 %fusion.7 = bf16[4,512,2048]{2,1,0:T(8,128)(2,1)S(1)} fusion(f32[2048]{0:T(1024)S(1)} %convert_element_type.103, bf16[4,512,4096]{2,1,0:T(8,128)(2,1)} %all-gather.15.cloned.1.call-done, bf16[4096,2048]{1,0:T(8,128)(2,1)} %param.28), kind=kOutput, calls=%fused_computation.9 | convolution fusion | flops 34401681408 | bytes 41951232 | tf_op jit(solution)/shard_map/bcd,df->bcf/dot_general | solution.py:278
  555.9 20.3 %fusion.36 = bf16[4,256,4096]{2,1,0:T(8,128)(2,1)S(1)} fusion(bf16[4,256,2048]{2,1,0:T(8,128)(2,1)S(1)} %bitcast.147, bf16[2048,4096]{1,0:T(8,128)(2,1)} %param.30), kind=kOutput, calls=%fused_computation.44 | convolution fusion | flops 17184063488 | bytes 29360128 | tf_op jit(solution)/shard_map/bce,ed->bcd/dot_general | solution.py:240
  576.5 14.4 %collective-permute-done.4 = bf16[4,256,4096]{2,1,0:T(8,128)(2,1)} collective-permute-done((bf16[4,256,4096]{2,1,0:T(8,128)(2,1)S(1)}, bf16[4,256,4096]{2,1,0:T(8,128)(2,1)}, u32[]{:S(2)}, u32[]{:S(2)}) %collective-permute-start.4) | collective-permute-done | bytes 8388640 | tf_op jit(solution)/shard_map/ppermute | solution.py:242
  590.9 24.5 %add_convert_fusion.1 = bf16[4,256,4096]{2,1,0:T(8,128)(2,1)} fusion(bf16[4,256,4096]{2,1,0:T(8,128)(2,1)} %collective-permute-done.4, bf16[4,256,2048]{2,1,0:T(8,128)(2,1)S(1)} %bitcast.145, bf16[2048,4096]{1,0:T(8,128)(2,1)} %param.30), kind=kOutput, calls=%fused_computation.31 | convolution fusion | flops 17192452096 | bytes 37748736 | tf_op jit(solution)/shard_map/bce,ed->bcd/dot_general | solution.py:240
  615.5 44.3 %fusion.15 = bf16[4,512,2048]{2,1,0:T(8,128)(2,1)S(1)} fusion(f32[2048]{0:T(1024)S(1)} %convert_element_type.103, bf16[4,512,4096]{2,1,0:T(8,128)(2,1)} %all-gather.17.cloned.1.call-done, bf16[4096,2048]{1,0:T(8,128)(2,1)} %param.28), kind=kOutput, calls=%fused_computation.17 | convolution fusion | flops 34401681408 | bytes 41951232 | tf_op jit(solution)/shard_map/bcd,df->bcf/dot_general | solution.py:278
  662.8 20.3 %fusion.39 = bf16[4,256,4096]{2,1,0:T(8,128)(2,1)S(1)} fusion(bf16[4,256,2048]{2,1,0:T(8,128)(2,1)S(1)} %bitcast.146, bf16[2048,4096]{1,0:T(8,128)(2,1)} %param.30), kind=kOutput, calls=%fused_computation.45 | convolution fusion | flops 17184063488 | bytes 29360128 | tf_op jit(solution)/shard_map/bce,ed->bcd/dot_general | solution.py:240
  683.4 12.9 %collective-permute-done.5 = bf16[4,256,4096]{2,1,0:T(8,128)(2,1)} collective-permute-done((bf16[4,256,4096]{2,1,0:T(8,128)(2,1)S(1)}, bf16[4,256,4096]{2,1,0:T(8,128)(2,1)}, u32[]{:S(2)}, u32[]{:S(2)}) %collective-permute-start.5) | collective-permute-done | bytes 8388640 | tf_op jit(solution)/shard_map/ppermute | solution.py:242
  696.3 24.5 %add_convert_fusion = bf16[4,256,4096]{2,1,0:T(8,128)(2,1)} fusion(bf16[4,256,4096]{2,1,0:T(8,128)(2,1)} %collective-permute-done.5, bf16[4,256,2048]{2,1,0:T(8,128)(2,1)S(1)} %bitcast.144, bf16[2048,4096]{1,0:T(8,128)(2,1)} %param.30), kind=kOutput, calls=%fused_computation.30 | convolution fusion | flops 17192452096 | bytes 37748736 | tf_op jit(solution)/shard_map/bce,ed->bcd/dot_general | solution.py:240
  764.5 37.1 %reduce-scatter.15.cloned.1.call-done.sum_ref = bf16[4,64,4096]{2,1,0:T(8,128)(2,1)} async-done(((bf16[4,256,4096]{2,1,0:T(8,128)(2,1)}), bf16[4,64,4096]{2,1,0:T(8,128)(2,1)}) %reduce-scatter.15.cloned.1.call-update) | async-done | bytes 2097168 | tf_op jit(solution)/shard_map/reduce_scatter | solution.py:246
  (147 shorter events, 135.7 us)
Async XLA Ops:
  7.2 56.9 %all-gather.13.cloned.1.call-start = ((), (), s32[]{:S(2)}) async-start(), calls=%async_computation.12 | async-start | bytes 9437184 | tf_op jit(solution)/shard_map/all_gather | solution.py:230
  12.8 102.1 %all-gather.11.cloned.1.call-start = ((), (), s32[]{:S(2)}) async-start(), calls=%async_computation.10 | async-start | bytes 9437184 | tf_op jit(solution)/shard_map/all_gather | solution.py:230
  15.8 180.1 %all-gather.9.cloned.1.call-start = ((), (), s32[]{:S(2)}) async-start(), calls=%async_computation.8 | async-start | bytes 9437184 | tf_op jit(solution)/shard_map/all_gather | solution.py:230
  18.9 203.2 %all-gather.7.cloned.1.call-start = ((), (), s32[]{:S(2)}) async-start(), calls=%async_computation.6 | async-start | bytes 9437184 | tf_op jit(solution)/shard_map/all_gather | solution.py:230
  21.9 321.9 %reduce-scatter.13.cloned.1.call-start = ((), (), s32[]{:S(2)}) async-start(), calls=%async_computation.13 | async-start | bytes 5242880 | tf_op jit(solution)/shard_map/reduce_scatter | solution.py:246
  134.0 37.4 %copy-start.2 = (bf16[2,512,512]{2,1,0:T(8,128)(2,1)S(1)}, bf16[2,512,512]{2,1,0:T(8,128)(2,1)}, u32[]{:S(2)}) copy-start(bf16[2,512,512]{2,1,0:T(8,128)(2,1)} %get-tuple-element.36) | copy-start | bytes 3145732
  177.5 7.2 collective-permute-start.3
  189.1 158.3 %reduce-scatter.11.cloned.1.call-start = ((), (), s32[]{:S(2)}) async-start(), calls=%async_computation.11 | async-start | bytes 5242880 | tf_op jit(solution)/shard_map/reduce_scatter | solution.py:246
  195.7 19.5 %collective-permute-start.2 = (bf16[2,256,4096]{2,1,0:T(8,128)(2,1)}, bf16[2,256,4096]{2,1,0:T(8,128)(2,1)}, u32[]{:S(2)}, u32[]{:S(2)}) collective-permute-start(bf16[2,256,4096]{2,1,0:T(8,128)(2,1)} %convolution_convert_fusion.1), channel_id=1, source_target_pairs={{0,1},{1,0},{2,3},{3,2},{4,5},{5,4},{6,7},{7,6}} | collective-permute-start | bytes 12582920 | tf_op jit(solution)/shard_map/ppermute | solution.py:242
  195.9 19.3 %copy-start.23 = (bf16[512,4096]{1,0:T(8,128)(2,1)S(1)}, bf16[512,4096]{1,0:T(8,128)(2,1)}, u32[]{:S(2)}) copy-start(bf16[512,4096]{1,0:T(8,128)(2,1)} %param.24) | copy-start | bytes 12582916
  222.0 150.4 %reduce-scatter.9.cloned.1.call-start = ((), (), s32[]{:S(2)}) async-start(), calls=%async_computation.9 | async-start | bytes 5242880 | tf_op jit(solution)/shard_map/reduce_scatter | solution.py:246
  273.2 34.5 %copy-start.3 = (bf16[2,512,512]{2,1,0:T(8,128)(2,1)S(1)}, bf16[2,512,512]{2,1,0:T(8,128)(2,1)}, u32[]{:S(2)}) copy-start(bf16[2,512,512]{2,1,0:T(8,128)(2,1)} %get-tuple-element.32) | copy-start | bytes 3145732
  313.8 7.2 collective-permute-start.1
  325.3 97.3 %reduce-scatter.7.cloned.1.call-start = ((), (), s32[]{:S(2)}) async-start(), calls=%async_computation.7 | async-start | bytes 5242880 | tf_op jit(solution)/shard_map/reduce_scatter | solution.py:246
  330.3 7.2 collective-permute-start
  341.9 166.7 %all-gather.15.cloned.1.call-start = ((), (), s32[]{:S(2)}) async-start(), calls=%async_computation.14 | async-start | bytes 18874368 | tf_op jit(solution)/shard_map/all_gather | solution.py:230
  354.0 75.8 %copy-start.21 = (bf16[2048]{0:T(1024)(128)(2,1)S(1)}, bf16[2048]{0:T(1024)(128)(2,1)}, u32[]{:S(2)}) copy-start(bf16[2048]{0:T(1024)(128)(2,1)} %param.29) | copy-start | bytes 12292
  354.0 261.4 %all-gather.17.cloned.1.call-start = ((), (), s32[]{:S(2)}) async-start(), calls=%async_computation.15 | async-start | bytes 18874368 | tf_op jit(solution)/shard_map/all_gather | solution.py:230
  429.3 330.7 %reduce-scatter.17.cloned.1.call-start = ((), (), s32[]{:S(2)}) async-start(), calls=%async_computation.17 | async-start | bytes 10485760 | tf_op jit(solution)/shard_map/reduce_scatter | solution.py:246
  555.9 35.0 %copy-start.1 = (bf16[4,4,1,64,2048]{4,3,2,1,0:T(8,128)(2,1)S(1)}, bf16[4,4,1,64,2048]{4,3,2,1,0:T(8,128)(2,1)}, u32[]{:S(2)}) copy-start(bf16[4,4,1,64,2048]{4,3,2,1,0:T(8,128)(2,1)} %get-tuple-element.60) | copy-start | bytes 12582916
  576.3 14.6 %collective-permute-start.4 = (bf16[4,256,4096]{2,1,0:T(8,128)(2,1)S(1)}, bf16[4,256,4096]{2,1,0:T(8,128)(2,1)}, u32[]{:S(2)}, u32[]{:S(2)}) collective-permute-start(bf16[4,256,4096]{2,1,0:T(8,128)(2,1)S(1)} %fusion.36), channel_id=1, source_target_pairs={{0,1},{1,0},{2,3},{3,2},{4,5},{5,4},{6,7},{7,6}} | collective-permute-start | bytes 25165832 | tf_op jit(solution)/shard_map/ppermute | solution.py:242
  615.4 186.1 %reduce-scatter.15.cloned.1.call-start = ((), (), s32[]{:S(2)}) async-start(), calls=%async_computation.16 | async-start | bytes 10485760 | tf_op jit(solution)/shard_map/reduce_scatter | solution.py:246
  662.8 33.5 %copy-start = (bf16[4,4,1,64,2048]{4,3,2,1,0:T(8,128)(2,1)S(1)}, bf16[4,4,1,64,2048]{4,3,2,1,0:T(8,128)(2,1)}, u32[]{:S(2)}) copy-start(bf16[4,4,1,64,2048]{4,3,2,1,0:T(8,128)(2,1)} %get-tuple-element.58) | copy-start | bytes 12582916
  683.1 13.1 %collective-permute-start.5 = (bf16[4,256,4096]{2,1,0:T(8,128)(2,1)S(1)}, bf16[4,256,4096]{2,1,0:T(8,128)(2,1)}, u32[]{:S(2)}, u32[]{:S(2)}) collective-permute-start(bf16[4,256,4096]{2,1,0:T(8,128)(2,1)S(1)} %fusion.39), channel_id=1, source_target_pairs={{0,1},{1,0},{2,3},{3,2},{4,5},{5,4},{6,7},{7,6}} | collective-permute-start | bytes 25165832 | tf_op jit(solution)/shard_map/ppermute | solution.py:242
  (20 other events, 151.0 us)
Sparse Core Ops, SparseCore 0:
  12.9 51.1 all-gather.12
  66.5 48.3 all-gather.10
  116.7 48.3 all-gather.8
  166.8 48.3 all-gather.6
  218.5 46.8 reduce-scatter.12
  268.1 46.8 reduce-scatter.10
  325.5 46.8 reduce-scatter.8
  375.8 46.8 reduce-scatter.6
  424.5 84.0 all-gather.14
  510.3 84.0 all-gather.16
  615.5 80.5 reduce-scatter.16
  721.0 80.5 reduce-scatter.14
